TPU v7x, 32 devices: a whole 2x2x4 slice. The times are simulated.
32 devices in a mesh: grp: 4 (over x, core), dev: 8 (over z, y).
Axes of the slice: x: 2, y: 2, z: 4, core: 2. Of those that a mesh axis runs over, the one named last changes fastest.
Arguments:
- points: bfloat16 [65536, 1024], P(('grp', 'dev')), may hold values from -6 to 6
- blocks: int32 [65536, 1], P(('grp', 'dev')), may hold values from 0 to 63; in each aligned block of 2048 rows (0 to 2047, 2048 to 4095, ...) at most 64 rows name the same one
- finals: int32 [65536], P(('grp', 'dev')), may hold values from 0 to 255
- centroids: bfloat16 [16384, 1024], P('dev'), may hold values from -6 to 6
Outputs:
- distances: bfloat16 [65536, 256], P(('grp', 'dev'))
- refreshed_centroids: float32 [16384, 1024], P('dev', 'grp')
Inputs may be any that keep to these rules, and one draw needn't show every extreme that they name: `blocks`: among the 2048 rows of one device no block is named by more than 64 rows, and some block by exactly 64. Block b is held by index b // 8 of dev. The point's centroid is row 256 * blocks + finals of centroids.
All inputs are finite; a program needn't handle non-finite values.
Results may differ from a plain program's by a relative error of at most 0.008.
Values may be sent and summed in bfloat16 or wider, within the bound.
A program may use at most 128 MiB of HBM per device.

v0:
```python
import jax
import jax.numpy as jnp
from jax import lax
from jax.sharding import PartitionSpec as P

BS = 256


def block_work(received_points, wanted, centroid_table, width, block_size):
    cent_norm = jnp.sum(jnp.square(centroid_table.astype(jnp.float32)), axis=-1)
    row_norm = jnp.sum(jnp.square(received_points.astype(jnp.float32)), axis=-1)
    cross_products = jnp.einsum(
        "nzy,nvy->nzv", received_points, centroid_table, preferred_element_type=jnp.float32
    )
    dists = ((row_norm[:, :, None] - 2.0 * cross_products + cent_norm[:, None, :]) / width).astype(
        jnp.bfloat16
    )
    onehot_assign = wanted[:, :, None] == jnp.arange(block_size, dtype=jnp.int32)[None, None, :]
    sums = jnp.einsum(
        "xnt,xni->xti",
        onehot_assign.astype(jnp.bfloat16),
        received_points,
        preferred_element_type=jnp.float32,
    )
    counts = jnp.sum(onehot_assign.astype(jnp.float32), axis=1)
    return (dists, sums, counts)


def shards(points, blocks, finals, centroids):
    shard_counts = lax.axis_size("dev")
    count_grp = lax.axis_size("grp")
    npoints, width = points.shape
    block_size = BS
    owned = centroids.shape[0] // block_size
    nblocks = owned * shard_counts
    depth = 2 * npoints // nblocks
    block_ids = blocks[:, 0]
    labels = jnp.arange(nblocks, dtype=jnp.int32)
    member = block_ids[:, None] == labels[None, :]
    lower = (jnp.arange(npoints)[:, None] > jnp.arange(npoints)[None, :]).astype(jnp.bfloat16)
    before = jnp.dot(lower, member.astype(jnp.bfloat16), preferred_element_type=jnp.float32)
    ranks = jnp.sum(jnp.where(member, before, 0.0), axis=1).astype(jnp.int32)
    share = width // count_grp
    slots = block_ids * depth + ranks
    outgoing = jnp.zeros((nblocks * depth, width), jnp.bfloat16).at[slots].set(points)
    targets = jnp.full((nblocks * depth,), -1, jnp.int32).at[slots].set(finals)
    outgoing = outgoing.reshape(nblocks, depth, width)
    targets = targets.reshape(nblocks, depth)
    received_points, wanted = (
        lax.all_to_all(outgoing, "dev", split_axis=0, concat_axis=1, tiled=True),
        lax.all_to_all(targets, "dev", split_axis=0, concat_axis=1, tiled=True),
    )
    centroid_table = centroids.reshape(owned, block_size, width)
    dists, sums, counts = block_work(received_points, wanted, centroid_table, width, block_size)
    sums = sums.reshape(owned * block_size, width)
    counts = counts.reshape(owned * block_size)
    returned = lax.all_to_all(dists, "dev", split_axis=1, concat_axis=0, tiled=True)
    distances = returned.reshape(nblocks * depth, block_size)[slots]
    col_sums = lax.psum_scatter(
        sums.astype(jnp.bfloat16), "grp", scatter_dimension=1, tiled=True
    ).astype(jnp.float32)
    all_counts = lax.psum(counts, "grp")
    own_cols = lax.dynamic_slice_in_dim(centroids, lax.axis_index("grp") * share, share, 1).astype(
        jnp.float32
    )
    refreshed_centroids = (col_sums + own_cols) / (all_counts + 1.0)[:, None]
    return (distances, refreshed_centroids)


def solution(mesh):
    placed = (P(("grp", "dev"), None), P(("grp", "dev"), None), P(("grp", "dev")), P("dev", None))
    return jax.shard_map(
        shards,
        mesh=mesh,
        in_specs=placed,
        out_specs=(P(("grp", "dev"), None), P("dev", "grp")),
        check_vma=False,
    )
```

profile of v0, /device:TPU:5, one launch (start us, length us, event | category | flops | bytes accessed | tf_op | source)
XLA Modules:
  0.0 337.6 jit_solution(2973195217341700019)
XLA Ops:
  7.2 0.0 copy-start.1
  7.2 2.5 fusion.7
  9.7 0.0 copy-done.1
  9.7 8.2 %scatter_custom_fusion.1 = s32[4096]{0:T(1024)S(1)} fusion(s32[2048]{0:T(1024)S(1)} %bitcast.28, s32[2048]{0:T(1024)} %param.6, s32[]{:T(128)} %constant.8.clone.1), kind=kCustom, calls=%fused_computation.21 | custom fusion | bytes 16896 | tf_op jit(solution)/shard_map/scatter | solution.py:46
  17.9 0.1 all_to_all.43
  18.0 0.7 reshape.73
  18.7 5.8 %all-to-all-start.2 = ((s32[8,1,512]{2,1,0:T(1,128)}), s32[8,1,512]{2,1,0:T(1,128)S(1)}, u32[]{:S(2)}, u32[]{:S(2)}) async-start(s32[8,1,512]{2,1,0:T(1,128)} %reshape.73), calls=%async_computation.2 | async-start | bytes 32768 | tf_op jit(solution)/shard_map/all_to_all | solution.py:51
  24.5 15.2 %scatter_custom_fusion = bf16[4096,1024]{1,0:T(8,128)(2,1)} fusion(s32[2048]{0:T(1024)S(1)} %bitcast.29, bf16[2048,1024]{1,0:T(8,128)(2,1)} %param.4, bf16[]{:T(256)} %constant.12.clone.1), kind=kCustom, calls=%fused_computation.11 | custom fusion | bytes 8389120 | tf_op jit(solution)/shard_map/scatter | solution.py:45
  39.7 0.0 all-to-all-done.2
  39.7 5.4 %all-to-all-start = ((bf16[64,64,1024]{2,1,0:T(8,128)(2,1)}), bf16[64,64,1024]{2,1,0:T(8,128)(2,1)}, u32[]{:S(2)}, u32[]{:S(2)}) async-start(bf16[64,64,1024]{2,1,0:T(8,128)(2,1)} %bitcast.21), calls=%async_computation | async-start | bytes 16777216 | tf_op jit(solution)/shard_map/all_to_all | solution.py:50
  45.1 0.0 reduce-scatter.2.cloned.1.call-start
  45.1 0.5 broadcast.19
  45.7 0.7 reduce.2
  46.3 0.1 reshape.74
  46.4 0.1 eq.34
  46.5 181.1 %all-to-all-done = bf16[64,64,1024]{2,1,0:T(8,128)(2,1)} async-done(((bf16[64,64,1024]{2,1,0:T(8,128)(2,1)}), bf16[64,64,1024]{2,1,0:T(8,128)(2,1)}, u32[]{:S(2)}, u32[]{:S(2)}) %all-to-all-start) | async-done | bytes 8388640 | tf_op jit(solution)/shard_map/all_to_all | solution.py:50
  227.6 8.4 %copy.17 = bf16[8,8,64,1024]{3,2,1,0:T(8,128)(2,1)} copy(bf16[8,8,64,1024]{3,2,0,1:T(8,128)(2,1)} %bitcast.5) | data formatting | bytes 16777216 | tf_op jit(solution)/shard_map/all_to_all | solution.py:50
  236.0 7.7 %fusion.4 = bf16[8,256,1024]{2,1,0:T(8,128)(2,1)} fusion(bf16[8,512,1024]{2,1,0:T(8,128)(2,1)} %bitcast.22, s32[8,512]{1,0:T(8,128)S(1)} %eq.34), kind=kOutput, calls=%fused_computation.13 | convolution fusion | flops 2150629376 | bytes 12599296 | tf_op jit(solution)/shard_map/xnt,xni->xti/dot_general | solution.py:19
  243.6 0.0 reduce-scatter.2.cloned.1.call-update
  243.7 3.1 multiply_reduce_fusion.1
  246.8 5.5 %multiply_reduce_fusion = f32[8,8,64]{2,0,1:T(8,128)S(1)} fusion(bf16[8,8,64,1024]{3,2,0,1:T(8,128)(2,1)} %bitcast.5), kind=kLoop, calls=%fused_computation.3 | loop fusion | flops 12578816 | bytes 8404992 | tf_op jit(solution)/shard_map/reduce_sum | solution.py:11
  252.3 0.1 sub.10
  252.4 7.9 %multiply_convert_fusion = bf16[8,512,256]{2,1,0:T(8,128)(2,1)S(1)} fusion(bf16[8,512,1024]{2,1,0:T(8,128)(2,1)} %bitcast.23, bf16[8,256,1024]{2,1,0:T(8,128)(2,1)} %bitcast.25, f32[8,256]{1,0:T(8,128)S(1)} %add.38, f32[8,512]{1,0:T(8,128)S(1)} %sub.10), kind=kOutput, calls=%fused_computation.10 | convolution fusion | flops 2152726528 | bytes 14704640 | tf_op jit(solution)/shard_map/nzy,nvy->nzv/dot_general | solution.py:12
  260.3 2.5 copy.18
  262.8 4.7 %all-to-all-start.1 = ((bf16[8,512,256]{2,0,1:T(8,128)(2,1)}), bf16[8,512,256]{2,0,1:T(8,128)(2,1)S(1)}, u32[]{:S(2)}, u32[]{:S(2)}) async-start(bf16[8,512,256]{2,0,1:T(8,128)(2,1)} %copy.18), calls=%async_computation.1 | async-start | bytes 4194304 | tf_op jit(solution)/shard_map/all_to_all | solution.py:57
  267.5 0.5 convert_reduce_fusion
  268.0 6.5 %psum.7 = f32[2048]{0:T(1024)S(1)} all-reduce(f32[2048]{0:T(1024)S(1)} %bitcast.33), channel_id=1, replica_groups=mesh['grp'=4,'dev'=8] {'grp'}, use_global_device_ids=true, to_apply=%region_7.8 | all-reduce | flops 2048 | bytes 16384 | tf_op jit(solution)/shard_map/psum | solution.py:62
  274.5 40.5 %all-to-all-done.1 = bf16[8,512,256]{2,0,1:T(8,128)(2,1)S(1)} async-done(((bf16[8,512,256]{2,0,1:T(8,128)(2,1)}), bf16[8,512,256]{2,0,1:T(8,128)(2,1)S(1)}, u32[]{:S(2)}, u32[]{:S(2)}) %all-to-all-start.1) | async-done | bytes 2097184 | tf_op jit(solution)/shard_map/all_to_all | solution.py:57
  315.0 0.0 copy-start
  315.0 1.3 copy-done
  316.3 2.1 copy.19
  318.5 9.1 %gather_fusion = bf16[2048,256]{1,0:T(8,128)(2,1)} fusion(bf16[4096,256]{1,0:T(8,128)(2,1)S(1)} %bitcast.20, s32[2048]{0:T(1024)S(1)} %broadcast_clamp_fusion), kind=kCustom, calls=%fused_computation | custom fusion | bytes 2105344 | tf_op jit(solution)/shard_map/gather | solution.py:58
  327.5 0.0 reduce-scatter.2.cloned.1.call-done
  327.5 3.2 add_divide_fusion
  (8 shorter events, 0.1 us)
Async XLA Ops:
  7.2 2.5 copy-start.1
  18.7 21.0 %all-to-all-start.2 = ((s32[8,1,512]{2,1,0:T(1,128)}), s32[8,1,512]{2,1,0:T(1,128)S(1)}, u32[]{:S(2)}, u32[]{:S(2)}) async-start(s32[8,1,512]{2,1,0:T(1,128)} %reshape.73), calls=%async_computation.2 | async-start | bytes 32768 | tf_op jit(solution)/shard_map/all_to_all | solution.py:51
  39.7 187.9 %all-to-all-start = ((bf16[64,64,1024]{2,1,0:T(8,128)(2,1)}), bf16[64,64,1024]{2,1,0:T(8,128)(2,1)}, u32[]{:S(2)}, u32[]{:S(2)}) async-start(bf16[64,64,1024]{2,1,0:T(8,128)(2,1)} %bitcast.21), calls=%async_computation | async-start | bytes 16777216 | tf_op jit(solution)/shard_map/all_to_all | solution.py:50
  45.1 282.4 %reduce-scatter.2.cloned.1.call-start = ((), (), s32[]{:S(2)}) async-start(), calls=%async_computation.4 | async-start | bytes 5242880 | tf_op jit(solution)/shard_map/reduce_scatter | solution.py:59
  262.8 52.2 %all-to-all-start.1 = ((bf16[8,512,256]{2,0,1:T(8,128)(2,1)}), bf16[8,512,256]{2,0,1:T(8,128)(2,1)S(1)}, u32[]{:S(2)}, u32[]{:S(2)}) async-start(bf16[8,512,256]{2,0,1:T(8,128)(2,1)} %copy.18), calls=%async_computation.1 | async-start | bytes 4194304 | tf_op jit(solution)/shard_map/all_to_all | solution.py:57
  315.0 1.3 copy-start
Sparse Core Ops, SparseCore 0:
  243.8 44.2 reduce-scatter.1
where the time goes:
time: 340 us; the launch traced here: 338 us
  waiting for transfers between devices  222 us (65%)
  local copies, waits for them, and re-layouts  48.4 us (14%)
  matrix products  18 us (5%)
  starting transfers between devices  15.9 us (5%)
  between operations  14.1 us (4%)
  other arithmetic  13 us (4%)
  blocking collectives  6.49 us (2%)
    all_to_all x1, waiting for transfers between devices, shards(): lax.all_to_all(outgoing, 'dev', split_axis=0, concat_axis=1, tiled=True)  181 us
    all_to_all x1, waiting for transfers between devices, shards(): lax.all_to_all(dists, 'dev', split_axis=1, concat_axis=0, tiled=True)  40.5 us
    scatter x1, local copies, waits for them, and re-layouts, shards(): jnp.zeros((nblocks * depth, width), jnp.bfloat16).at[slots].set(points)  15.2 us
    gather x1, local copies, waits for them, and re-layouts, shards(): distances = returned.reshape(nblocks * depth, block_size)[slots]  9.06 us
    all_to_all x1, local copies, waits for them, and re-layouts, shards(): lax.all_to_all(outgoing, 'dev', split_axis=0, concat_axis=1, tiled=True)  8.39 us
    scatter x1, local copies, waits for them, and re-layouts, shards(): targets = jnp.full((nblocks * depth,), -1, jnp.int32).at[slots].set(finals)  8.23 us
    dot_general x1, matrix products, block_work(): jnp.einsum('nzy,nvy->nzv', received_points, centroid_table, preferred_ele...  7.9 us
    dot_general x1, matrix products, block_work(): jnp.einsum('xnt,xni->xti', onehot_assign.astype(jnp.bfloat16), received_p...  7.66 us
  transfers between devices with their start and end apart: 4, of which 2 were waited for; matrix products, arithmetic and copies ran while one was open for 14% of the time, Pallas kernels for 0%

commit v1 on v0

--- a/solution.py
+++ b/solution.py
@@ -27,42 +27,66 @@
 
 
 def shards(points, blocks, finals, centroids):
-    shard_counts = lax.axis_size("dev")
-    count_grp = lax.axis_size("grp")
+    n_dev = lax.axis_size("dev")
+    n_grp = lax.axis_size("grp")
+    halves = 2 if n_dev % 2 == 0 else 1
+    team = n_dev // halves
+    groups = [[h * team + s for s in range(team)] for h in range(halves)]
+    swap = [(d, (d + team) % n_dev) for d in range(n_dev)]
+    half = lax.axis_index("dev") // team
     npoints, width = points.shape
     block_size = BS
-    owned = centroids.shape[0] // block_size
-    nblocks = owned * shard_counts
+    rows = centroids.shape[0]
+    owned = rows // block_size
+    nblocks = owned * n_dev
     depth = 2 * npoints // nblocks
+    share = width // n_grp
+    part = rows // n_grp
+    me_grp = lax.axis_index("grp")
+
+    mine = lax.dynamic_slice_in_dim(centroids, me_grp * part, part, 0)
+    crossed = lax.ppermute(mine, "dev", swap)
+    others = lax.all_gather(crossed, "grp", axis=0, tiled=True)
+
     block_ids = blocks[:, 0]
     labels = jnp.arange(nblocks, dtype=jnp.int32)
     member = block_ids[:, None] == labels[None, :]
     lower = (jnp.arange(npoints)[:, None] > jnp.arange(npoints)[None, :]).astype(jnp.bfloat16)
     before = jnp.dot(lower, member.astype(jnp.bfloat16), preferred_element_type=jnp.float32)
     ranks = jnp.sum(jnp.where(member, before, 0.0), axis=1).astype(jnp.int32)
-    share = width // count_grp
-    slots = block_ids * depth + ranks
+    holder = block_ids // owned
+    other = (holder // team) ^ half if halves == 2 else 0
+    place = ((holder % team) * halves + other) * owned + block_ids % owned
+    slots = place * depth + ranks
     outgoing = jnp.zeros((nblocks * depth, width), jnp.bfloat16).at[slots].set(points)
     targets = jnp.full((nblocks * depth,), -1, jnp.int32).at[slots].set(finals)
     outgoing = outgoing.reshape(nblocks, depth, width)
     targets = targets.reshape(nblocks, depth)
-    received_points, wanted = (
-        lax.all_to_all(outgoing, "dev", split_axis=0, concat_axis=1, tiled=True),
-        lax.all_to_all(targets, "dev", split_axis=0, concat_axis=1, tiled=True),
-    )
-    centroid_table = centroids.reshape(owned, block_size, width)
-    dists, sums, counts = block_work(received_points, wanted, centroid_table, width, block_size)
-    sums = sums.reshape(owned * block_size, width)
-    counts = counts.reshape(owned * block_size)
-    returned = lax.all_to_all(dists, "dev", split_axis=1, concat_axis=0, tiled=True)
+
+    def exchange(x, split, join):
+        return lax.all_to_all(
+            x, "dev", split_axis=split, concat_axis=join, tiled=True, axis_index_groups=groups
+        )
+
+    received_points, wanted = exchange(outgoing, 0, 1), exchange(targets, 0, 1)
+    table = jnp.concatenate([centroids, others], axis=0) if halves == 2 else centroids
+    table = table.reshape(halves * owned, block_size, width)
+    dists, sums, counts = block_work(received_points, wanted, table, width, block_size)
+    returned = exchange(dists, 1, 0)
     distances = returned.reshape(nblocks * depth, block_size)[slots]
-    col_sums = lax.psum_scatter(
-        sums.astype(jnp.bfloat16), "grp", scatter_dimension=1, tiled=True
-    ).astype(jnp.float32)
-    all_counts = lax.psum(counts, "grp")
-    own_cols = lax.dynamic_slice_in_dim(centroids, lax.axis_index("grp") * share, share, 1).astype(
-        jnp.float32
-    )
+    sums = sums.reshape(halves * rows, width).astype(jnp.bfloat16)
+    counts = counts.reshape(halves * rows)
+    if halves == 2:
+        far = lax.psum_scatter(sums[rows:], "grp", scatter_dimension=1, tiled=True)
+        far = lax.ppermute(far, "dev", swap)
+        near = lax.psum_scatter(sums[:rows], "grp", scatter_dimension=1, tiled=True)
+        col_sums = near.astype(jnp.float32) + far.astype(jnp.float32)
+        all_counts = lax.psum(counts, "grp")
+        all_counts = all_counts[:rows] + lax.ppermute(all_counts[rows:], "dev", swap)
+    else:
+        col_sums = lax.psum_scatter(sums, "grp", scatter_dimension=1, tiled=True).astype(jnp.float32)
+        all_counts = lax.psum(counts, "grp")
+    own_cols = lax.dynamic_slice_in_dim(centroids, me_grp * share, share, 1).astype(jnp.float32)
     refreshed_centroids = (col_sums + own_cols) / (all_counts + 1.0)[:, None]
     return (distances, refreshed_centroids)
 

time: 340 us -> 315 us (0.926)
  waiting for transfers between devices: 222 us -> 170 us
  local copies, waits for them, and re-layouts: 48.4 us -> 63.9 us
  blocking collectives: 6.49 us -> 10 us
    all_to_all x3, waiting for transfers between devices: 222 us -> 0.01 us  [exchange(): lax.all_to_all(x, 'dev', split_axis=split, concat_axis=join, tiled=True,...]
    ppermute x0 -> x3, waiting for transfers between devices: none -> 143 us  [the longest x1 108 us: shards(): crossed = lax.ppermute(mine, 'dev', swap)]
    reduce_scatter x1 -> x2, waiting for transfers between devices: 0.01 us -> 14.6 us  [the longest x1 14.6 us: shards(): far = lax.psum_scatter(sums[rows:], 'grp', scatter_dimension=1, tiled=True)]
    all_gather x0 -> x1, waiting for transfers between devices: none -> 12.3 us  [shards(): others = lax.all_gather(crossed, 'grp', axis=0, tiled=True)]
    unnamed x7 -> x10, local copies, waits for them, and re-layouts: 2.1 us -> 7.67 us
    ppermute x0 -> x3, starting transfers between devices: none -> 4.73 us  [the longest x1 2.36 us: shards(): crossed = lax.ppermute(mine, 'dev', swap)]
    concatenate x0 -> x1, local copies, waits for them, and re-layouts: none -> 4.59 us  [shards(): jnp.concatenate([centroids, others], axis=0)]
    slice x0 -> x2, local copies, waits for them, and re-layouts: none -> 3.75 us  [the longest x1 3.74 us: shards(): near = lax.psum_scatter(sums[:rows], 'grp', scatter_dimension=1, tiled=True)]
  transfers between devices with their start and end apart: 4 -> 9, of which waited for: 2 -> 4; matrix products, arithmetic and copies ran while one was open for 14% -> 26% of each run, Pallas kernels for 0% -> 0%
where the time goes in v1:
time: 315 us; the launch traced here: 311 us
  waiting for transfers between devices  170 us (54%)
  local copies, waits for them, and re-layouts  63.9 us (20%)
  matrix products  18.6 us (6%)
  starting transfers between devices  18.2 us (6%)
  other arithmetic  16.2 us (5%)
  between operations  13.9 us (4%)
  blocking collectives  10 us (3%)
    ppermute x1, waiting for transfers between devices, shards(): crossed = lax.ppermute(mine, 'dev', swap)  108 us
    ppermute x1, waiting for transfers between devices, shards(): lax.ppermute(all_counts[rows:], 'dev', swap)  34.8 us
    scatter x1, local copies, waits for them, and re-layouts, shards(): jnp.zeros((nblocks * depth, width), jnp.bfloat16).at[slots].set(points)  15.2 us
    reduce_scatter x1, waiting for transfers between devices, shards(): far = lax.psum_scatter(sums[rows:], 'grp', scatter_dimension=1, tiled=True)  14.6 us
    all_to_all x3, starting transfers between devices, exchange(): lax.all_to_all(x, 'dev', split_axis=split, concat_axis=join, tiled=True,...  13.2 us
    all_gather x1, waiting for transfers between devices, shards(): others = lax.all_gather(crossed, 'grp', axis=0, tiled=True)  12.3 us
    all_to_all x5, local copies, waits for them, and re-layouts, exchange(): lax.all_to_all(x, 'dev', split_axis=split, concat_axis=join, tiled=True,...  11.4 us
    psum x1, blocking collectives, shards(): all_counts = lax.psum(counts, 'grp')  10 us
  transfers between devices with their start and end apart: 9, of which 4 were waited for; matrix products, arithmetic and copies ran while one was open for 26% of the time, Pallas kernels for 0%

profile of v1, /device:TPU:5, one launch (start us, length us, event | category | flops | bytes accessed | tf_op | source)
XLA Modules:
  0.0 311.2 jit_solution(5527898152115321221)
XLA Ops:
  7.2 0.0 copy-start.2
  7.2 2.5 fusion.5
  9.7 0.0 copy-done.2
  9.7 0.1 compare_select_fusion
  9.8 8.2 %scatter_custom_fusion.1 = s32[4096]{0:T(1024)S(1)} fusion(s32[2048]{0:T(1024)S(1)} %bitcast.32, s32[2048]{0:T(1024)} %param.6, s32[]{:T(128)} %constant.76.clone.1), kind=kCustom, calls=%fused_computation.35 | custom fusion | bytes 16896 | tf_op jit(solution)/shard_map/scatter | solution.py:62
  18.1 0.1 all_to_all.43
  18.1 0.7 reshape.75
  18.8 3.8 %all-to-all-start.2 = ((s32[4,1,1024]{2,1,0:T(1,128)}), s32[4,1,1024]{2,1,0:T(1,128)S(1)}, u32[]{:S(2)}, u32[]{:S(2)}) async-start(s32[4,1,1024]{2,1,0:T(1,128)} %reshape.75), calls=%async_computation.2 | async-start | bytes 32768 | tf_op jit(solution)/shard_map/all_to_all | solution.py:67
  22.6 15.2 %scatter_custom_fusion = bf16[4096,1024]{1,0:T(8,128)(2,1)} fusion(s32[2048]{0:T(1024)S(1)} %bitcast.33, bf16[2048,1024]{1,0:T(8,128)(2,1)} %param.4, bf16[]{:T(256)} %constant.71.clone.1), kind=kCustom, calls=%fused_computation.11 | custom fusion | bytes 8389120 | tf_op jit(solution)/shard_map/scatter | solution.py:61
  37.8 0.0 all-to-all-done.2
  37.8 5.6 %all-to-all-start = ((bf16[64,64,1024]{2,1,0:T(8,128)(2,1)}), bf16[64,64,1024]{2,1,0:T(8,128)(2,1)}, u32[]{:S(2)}, u32[]{:S(2)}) async-start(bf16[64,64,1024]{2,1,0:T(8,128)(2,1)} %bitcast.24), calls=%async_computation | async-start | bytes 16777216 | tf_op jit(solution)/shard_map/all_to_all | solution.py:67
  43.4 0.0 all-gather.2.cloned.1.call-start
  43.5 1.3 constant_dynamic-slice_fusion
  44.8 2.4 collective-permute-start
  47.1 108.0 %collective-permute-done = bf16[512,1024]{1,0:T(8,128)(2,1)S(1)} collective-permute-done((bf16[512,1024]{1,0:T(8,128)(2,1)S(1)}, bf16[512,1024]{1,0:T(8,128)(2,1)S(1)}, u32[]{:S(2)}, u32[]{:S(2)}) %collective-permute-start) | collective-permute-done | bytes 1048608 | tf_op jit(solution)/shard_map/ppermute | solution.py:48
  155.1 0.0 copy-start.1
  155.1 1.0 copy-done.1
  156.1 0.0 all-gather.2.cloned.1.call-update
  156.1 0.2 reduce-scatter.5.cloned.1.call-start
  156.4 0.5 broadcast.62
  156.9 0.7 reduce.2
  157.6 0.1 reshape.76
  157.7 0.1 eq.37
  157.8 0.0 all-to-all-done
  157.8 8.4 %copy.17 = bf16[16,4,64,1024]{3,2,1,0:T(8,128)(2,1)} copy(bf16[16,4,64,1024]{3,2,0,1:T(8,128)(2,1)} %bitcast.5) | data formatting | bytes 16777216 | tf_op jit(solution)/shard_map/all_to_all | solution.py:67
  166.2 6.8 %convolution_convert_fusion = bf16[16,256,1024]{2,1,0:T(8,128)(2,1)S(1)} fusion(bf16[16,256,1024]{2,1,0:T(8,128)(2,1)} %bitcast.21, s32[16,256]{1,0:T(8,128)S(1)} %eq.37), kind=kOutput, calls=%fused_computation.7 | convolution fusion | flops 2152726528 | bytes 16793600 | tf_op jit(solution)/shard_map/xnt,xni->xti/dot_general | solution.py:19
  173.0 3.7 %fusion.13 = (bf16[8,256,1024]{2,1,0:T(8,128)(2,1)}, bf16[8,256,1024]{2,1,0:T(8,128)(2,1)}) fusion(bf16[16,256,1024]{2,1,0:T(8,128)(2,1)S(1)} %convolution_convert_fusion), kind=kLoop, calls=%fused_computation.41 | loop fusion | bytes 16777216 | tf_op jit(solution)/shard_map/slice | solution.py:82
  176.7 0.0 reduce-scatter.5.cloned.1.call-update
  176.8 0.0 reduce-scatter.3.cloned.1.call-start
  176.8 0.7 reduce-scatter.3.cloned.1.call-update
  177.5 4.6 %constant_dynamic-update-slice_fusion.1 = bf16[4096,1024]{1,0:T(8,128)(2,1)} fusion(bf16[2048,1024]{1,0:T(8,128)(2,1)} %param.7), kind=kLoop, calls=%fused_computation.39 | loop fusion | bytes 8388608
  182.1 12.3 %all-gather.2.cloned.1.call-done = bf16[2048,1024]{1,0:T(8,128)(2,1)} async-done(((bf16[512,1024]{1,0:T(8,128)(2,1)}), bf16[2048,1024]{1,0:T(8,128)(2,1)}) %all-gather.2.cloned.1.call-update) | async-done | bytes 4194320 | tf_op jit(solution)/shard_map/all_gather | solution.py:49
  194.4 4.6 %constant_dynamic-update-slice_fusion = bf16[4096,1024]{1,0:T(8,128)(2,1)} fusion(bf16[4096,1024]{1,0:T(8,128)(2,1)} %constant_dynamic-update-slice_fusion.1, bf16[2048,1024]{1,0:T(8,128)(2,1)} %all-gather.2.cloned.1.call-done), kind=kLoop, calls=%fused_computation.38 | loop fusion | bytes 8388608 | tf_op jit(solution)/shard_map/concatenate | solution.py:72
  199.0 5.1 %multiply_reduce_fusion = f32[4096]{0:T(1024)S(1)} fusion(bf16[4096,1024]{1,0:T(8,128)(2,1)} %constant_dynamic-update-slice_fusion), kind=kLoop, calls=%fused_computation.3 | loop fusion | flops 12578816 | bytes 8404992 | tf_op jit(solution)/shard_map/reduce_sum | solution.py:10
  204.1 6.3 %multiply_reduce_fusion.1 = f32[16,4,64]{2,0,1:T(8,128)S(1)} fusion(bf16[16,4,64,1024]{3,2,0,1:T(8,128)(2,1)} %bitcast.5), kind=kLoop, calls=%fused_computation.4 | loop fusion | flops 12578816 | bytes 8404992 | tf_op jit(solution)/shard_map/reduce_sum | solution.py:11
  210.5 0.1 sub.27
  210.5 9.3 %multiply_convert_fusion = bf16[16,256,256]{2,1,0:T(8,128)(2,1)S(1)} fusion(f32[16,256]{1,0:T(8,128)S(1)} %add.79, f32[16,256]{1,0:T(8,128)S(1)} %sub.27, bf16[16,256,1024]{2,1,0:T(8,128)(2,1)} %bitcast.22, bf16[16,256,1024]{2,1,0:T(8,128)(2,1)} %bitcast.25), kind=kOutput, calls=%fused_computation.10 | convolution fusion | flops 2152726528 | bytes 18907136 | tf_op jit(solution)/shard_map/nzy,nvy->nzv/dot_general | solution.py:12
  219.8 2.5 copy.18
  222.3 3.8 %all-to-all-start.1 = ((bf16[16,256,256]{2,0,1:T(8,128)(2,1)}), bf16[16,256,256]{2,0,1:T(8,128)(2,1)S(1)}, u32[]{:S(2)}, u32[]{:S(2)}) async-start(bf16[16,256,256]{2,0,1:T(8,128)(2,1)} %copy.18), calls=%async_computation.1 | async-start | bytes 4194304 | tf_op jit(solution)/shard_map/all_to_all | solution.py:67
  226.2 14.6 %reduce-scatter.5.cloned.1.call-done = bf16[2048,256]{1,0:T(8,128)(2,1)} async-done(((bf16[2048,1024]{1,0:T(8,128)(2,1)}), bf16[2048,256]{1,0:T(8,128)(2,1)}) %reduce-scatter.5.cloned.1.call-update) | async-done | bytes 1048592 | tf_op jit(solution)/shard_map/reduce_scatter | solution.py:80
  240.8 2.1 collective-permute-start.1
  242.9 0.6 convert_reduce_fusion
  243.5 10.0 %psum.7 = f32[4096]{0:T(1024)S(1)} all-reduce(f32[4096]{0:T(1024)S(1)} %bitcast.31), channel_id=1, replica_groups=mesh['grp'=4,'dev'=8] {'grp'}, use_global_device_ids=true, to_apply=%region_8.9 | all-reduce | flops 4096 | bytes 32768 | tf_op jit(solution)/shard_map/psum | solution.py:84
  253.6 0.2 collective-permute-start.2
  253.8 34.8 %collective-permute-done.2 = f32[2048]{0:T(1024)S(1)} collective-permute-done((f32[2048]{0:T(1024)S(1)}, f32[2048]{0:T(1024)S(1)}, u32[]{:S(2)}, u32[]{:S(2)}) %collective-permute-start.2) | collective-permute-done | bytes 8224 | tf_op jit(solution)/shard_map/ppermute | solution.py:85
  288.6 0.0 all-to-all-done.1
  288.6 0.0 copy-start
  288.6 1.3 copy-done
  290.0 2.4 copy.19
  292.3 9.1 %gather_fusion = bf16[2048,256]{1,0:T(8,128)(2,1)} fusion(bf16[4096,256]{1,0:T(8,128)(2,1)S(1)} %bitcast.23, s32[2048]{0:T(1024)S(1)} %broadcast_clamp_fusion), kind=kCustom, calls=%fused_computation | custom fusion | bytes 2105344 | tf_op jit(solution)/shard_map/gather | solution.py:76
  301.4 0.0 reduce-scatter.3.cloned.1.call-done
  301.4 0.0 collective-permute-done.1
  301.4 3.3 %add_divide_fusion = f32[2048,256]{1,0:T(8,128)} fusion(bf16[2048,256]{1,0:T(8,128)(2,1)S(1)} %collective-permute-done.1, bf16[2048,256]{1,0:T(8,128)(2,1)} %reduce-scatter.3.cloned.1.call-done, f32[2048]{0:T(1024)S(1)} %fusion.10, bf16[2048,1024]{1,0:T(8,128)(2,1)} %param.7, s32[]{:T(128)S(6)} %select_n.51), kind=kLoop, calls=%fused_computation.14 | loop fusion | flops 3145728 | bytes 5251076 | tf_op jit(solution)/shard_map/div | solution.py:90
  (8 shorter events, 0.1 us)
Async XLA Ops:
  7.2 2.5 copy-start.2
  18.8 19.0 %all-to-all-start.2 = ((s32[4,1,1024]{2,1,0:T(1,128)}), s32[4,1,1024]{2,1,0:T(1,128)S(1)}, u32[]{:S(2)}, u32[]{:S(2)}) async-start(s32[4,1,1024]{2,1,0:T(1,128)} %reshape.75), calls=%async_computation.2 | async-start | bytes 32768 | tf_op jit(solution)/shard_map/all_to_all | solution.py:67
  37.8 119.9 %all-to-all-start = ((bf16[64,64,1024]{2,1,0:T(8,128)(2,1)}), bf16[64,64,1024]{2,1,0:T(8,128)(2,1)}, u32[]{:S(2)}, u32[]{:S(2)}) async-start(bf16[64,64,1024]{2,1,0:T(8,128)(2,1)} %bitcast.24), calls=%async_computation | async-start | bytes 16777216 | tf_op jit(solution)/shard_map/all_to_all | solution.py:67
  43.4 151.0 %all-gather.2.cloned.1.call-start = ((), (), s32[]{:S(2)}) async-start(), calls=%async_computation.5 | async-start | bytes 5242880 | tf_op jit(solution)/shard_map/all_gather | solution.py:49
  44.8 110.4 %collective-permute-start = (bf16[512,1024]{1,0:T(8,128)(2,1)S(1)}, bf16[512,1024]{1,0:T(8,128)(2,1)S(1)}, u32[]{:S(2)}, u32[]{:S(2)}) collective-permute-start(bf16[512,1024]{1,0:T(8,128)(2,1)S(1)} %constant_dynamic-slice_fusion), channel_id=1, source_target_pairs={{0,4},{1,5},{2,6},{3,7},{4,0},{5,1},{6,2},{7,3},{8,12},{9,13},{10,... | collective-permute-start | bytes 3145736 | tf_op jit(solution)/shard_map/ppermute | solution.py:48
  155.1 1.0 copy-start.1
  156.1 84.6 %reduce-scatter.5.cloned.1.call-start = ((), (), s32[]{:S(2)}) async-start(), calls=%async_computation.7 | async-start | bytes 5242880 | tf_op jit(solution)/shard_map/reduce_scatter | solution.py:80
  176.8 124.6 %reduce-scatter.3.cloned.1.call-start = ((), (), s32[]{:S(2)}) async-start(), calls=%async_computation.6 | async-start | bytes 5242880 | tf_op jit(solution)/shard_map/reduce_scatter | solution.py:82
  222.3 66.3 %all-to-all-start.1 = ((bf16[16,256,256]{2,0,1:T(8,128)(2,1)}), bf16[16,256,256]{2,0,1:T(8,128)(2,1)S(1)}, u32[]{:S(2)}, u32[]{:S(2)}) async-start(bf16[16,256,256]{2,0,1:T(8,128)(2,1)} %copy.18), calls=%async_computation.1 | async-start | bytes 4194304 | tf_op jit(solution)/shard_map/all_to_all | solution.py:67
  240.8 60.6 %collective-permute-start.1 = (bf16[2048,256]{1,0:T(8,128)(2,1)}, bf16[2048,256]{1,0:T(8,128)(2,1)S(1)}, u32[]{:S(2)}, u32[]{:S(2)}) collective-permute-start(bf16[2048,256]{1,0:T(8,128)(2,1)} %reduce-scatter.5.cloned.1.call-done), channel_id=1, source_target_pairs={{0,4},{1,5},{2,6},{3,7},{4,0},{5,1},{6,2},{7,3},{8,12},{9,13},{10,... | collective-permute-start | bytes 3145736 | tf_op jit(solution)/shard_map/ppermute | solution.py:81
  253.6 35.1 %collective-permute-start.2 = (f32[2048]{0:T(1024)S(1)}, f32[2048]{0:T(1024)S(1)}, u32[]{:S(2)}, u32[]{:S(2)}) collective-permute-start(f32[2048]{0:T(1024)S(1)} %slice.29), channel_id=1, source_target_pairs={{0,4},{1,5},{2,6},{3,7},{4,0},{5,1},{6,2},{7,3},{8,12},{9,13},{10,... | collective-permute-start | bytes 24584 | tf_op jit(solution)/shard_map/ppermute | solution.py:85
  288.6 1.3 copy-start
Sparse Core Ops, SparseCore 0:
  156.3 38.0 all-gather.1
  196.9 43.8 reduce-scatter.4
  243.3 44.3 reduce-scatter.2

commit v2 on v0

v2 whole, which is shorter than its diff:
```python
import functools

import jax
import jax.numpy as jnp
from jax import lax
from jax.experimental import pallas as pl
from jax.experimental.pallas import tpu as pltpu
from jax.sharding import PartitionSpec as P

BS = 256
MESH = pl.DeviceIdType.MESH
F32, BF16 = jnp.float32, jnp.bfloat16


def kernel(
    n_grp, n_dev, owned, depth,
    slot_row, slot_col, final_row, points, cent, cn_own,
    distances, col_sums, counts_out,
    out, recv, tgt_out, tgt_in, tgt_col, others, cn_oth,
    part, pair_in, x_in, fin, mid_in, dist, ret,
    cnt, cnt_in, cnt_fin, cnt_mid,
    s_pts, r_pts, s_tgt, r_tgt, s_cen, r_cen, s_fwd, r_fwd, s_cn, r_cn,
    s_pair, r_pair, s_x, r_x, s_mid, r_mid, s_cnt, r_cnt, s_cm, r_cm, s_ret, r_ret, l_sem,
):
    team = n_dev // 2
    n_x = n_grp // 2
    g, d = lax.axis_index("grp"), lax.axis_index("dev")
    x, c = g // 2, g % 2
    half, me = d // team, d % team
    npts, width = points.shape
    rows = cent.shape[0]
    share = width // n_grp
    piece = rows // n_grp
    n_cut = 2
    pc = piece // n_cut
    per = owned * depth
    tile = min(256, per)
    nb = tile // depth

    def to(gg, dd):
        return {"grp": gg, "dev": dd}

    def mate(o):
        return half * team + (me + o) % team

    def copy(src, dst, ss, rs, dev):
        return pltpu.make_async_remote_copy(
            src_ref=src, dst_ref=dst, send_sem=ss, recv_sem=rs, device_id=dev, device_id_type=MESH
        )

    swap = to(g, (d + team) % n_dev)
    barrier = pltpu.get_barrier_semaphore()
    peers = [to(g, mate(o)) for o in range(1, team)] + [swap]
    peers += [to((g + o) % n_grp, d) for o in range(1, n_grp)]
    for p in peers:
        pl.semaphore_signal(barrier, inc=1, device_id=p, device_id_type=MESH)
    pl.semaphore_wait(barrier, len(peers))

    def span(gg, j):
        return pl.ds(pl.multiple_of(gg * piece + j * pc, pc), pc)

    cen = [copy(cent.at[span(g, j)], others.at[span(g, j)], s_cen.at[j], r_cen.at[j], swap) for j in range(n_cut)]
    cnc = copy(cn_own, cn_oth, s_cn.at[0], r_cn.at[0], swap)
    for j in range(n_cut):
        cen[j].start()
    cnc.start()

    fwd = [
        copy(others.at[span(g, j)], others.at[span(g, j)], s_fwd.at[j, o], r_fwd.at[j, o], to((g + o) % n_grp, d))
        for j in range(n_cut)
        for o in range(1, n_grp)
    ]

    def packed(h, who, t):
        base = ((who * 2 + h) * owned) * depth + t * tile
        hot = (lax.broadcasted_iota(jnp.int32, (tile, npts), 0) + base == slot_row[...]).astype(BF16)
        pts = jnp.dot(hot, points[...], preferred_element_type=F32).astype(BF16)
        tg = lax.dot_general(final_row[...], hot, (((1,), (1,)), ((), ())), preferred_element_type=F32)
        return pts.reshape(nb, depth, width), tg

    mine = pl.ds(pl.multiple_of(me * depth, depth), depth)
    pts_c, tgt_c = {}, {}
    for h in (1, 0):
        for o in range(1, team):
            pts_c[h, o] = copy(out.at[h, o - 1], recv.at[h, :, mine], s_pts.at[h, o], r_pts.at[h, o], to(g, mate(o)))
            tgt_c[h, o] = copy(tgt_out.at[h, o - 1], tgt_in.at[h, o - 1], s_tgt.at[h, o], r_tgt.at[h, o], to(g, mate(o)))

    def pack_all(h):
        for o in range(1, team):
            for t in range(per // tile):
                pts, tg = packed(h, (me + o) % team, t)
                out[h, o - 1, t * nb : (t + 1) * nb] = pts
                tgt_out[h, o - 1, :, t * tile : (t + 1) * tile] = tg
            pts_c[h, o].start()
            tgt_c[h, o].start()

    def put_targets(h, src, tg):
        col = jnp.transpose(tg)
        tgt_col[h, :, pl.ds(pl.multiple_of(src * depth, depth), depth), :] = col.reshape(-1, depth, 8)

    def pack_own(h):
        for t in range(per // tile):
            pts, tg = packed(h, me, t)
            recv[h, t * nb : (t + 1) * nb, mine] = pts
            tgt_col[h, t * nb : (t + 1) * nb, mine, :] = jnp.transpose(tg).reshape(nb, depth, 8)

    def forward(j):
        cen[j].wait_recv()
        for o in range(1, n_grp):
            fwd[j * (n_grp - 1) + o - 1].start()

    pack_all(1)
    pack_own(1)
    forward(0)
    pack_all(0)
    pack_own(0)
    for j in range(1, n_cut):
        forward(j)

    pair_c = {
        (h, xx): copy(part.at[h, xx * 2 + 1 - c], pair_in.at[h, xx], s_pair.at[h, xx], r_pair.at[h, xx], to(x * 2 + 1 - c, d))
        for h in (1, 0)
        for xx in range(n_x)
    }
    x_c = {
        (h, o): copy(part.at[h, (x + o) % n_x * 2 + c], x_in.at[h, o - 1], s_x.at[h, o], r_x.at[h, o], to((x + o) % n_x * 2 + c, d))
        for h in (1, 0)
        for o in range(1, n_x)
    }
    ret_c = {
        (h, o): copy(dist.at[h, :, pl.ds(pl.multiple_of((me + o) % team * depth, depth), depth)],
                     ret.at[h, me], s_ret.at[h, o], r_ret.at[h, o], to(g, mate(o)))
        for h in (1, 0)
        for o in range(1, team)
    }
    cnt_c = {
        o: copy(cnt, cnt_in.at[o - 1], s_cnt.at[o], r_cnt.at[o], to((g + o) % n_grp, d)) for o in range(1, n_grp)
    }
    mid_c = copy(fin, mid_in, s_mid.at[0], r_mid.at[0], swap)
    cm_c = copy(cnt_fin.at[1], cnt_mid, s_cm.at[0], r_cm.at[0], swap)

    def sums(h):
        for o in range(1, team):
            pts_c[h, o].wait_recv()
            tgt_c[h, o].wait_recv()
            put_targets(h, (me + team - o) % team, tgt_in[h, o - 1])

        @pl.loop(0, owned)
        def _(b):
            want = tgt_col[h, b][:, 0:1].astype(jnp.int32) - 1
            hot = (lax.broadcasted_iota(jnp.int32, (team * depth, BS), 1) == want).astype(F32)
            cnt[h, pl.ds(b, 1), :] = jnp.sum(hot, axis=0, keepdims=True)
            s = lax.dot_general(hot.astype(BF16), recv[h, b], (((0,), (0,)), ((), ())), preferred_element_type=F32)
            s = s.astype(BF16)
            here = pl.ds(pl.multiple_of(b * BS, BS), BS)
            for k in range(n_grp):
                part[h, k, here, :] = s[:, k * share : (k + 1) * share]

        for xx in range(n_x):
            pair_c[h, xx].start()

    def pair(h):
        for xx in range(n_x):
            pair_c[h, xx].wait_recv()
        for o in list(range(1, n_x)) + [0]:
            xx = (x + o) % n_x

            @pl.loop(0, rows // BS)
            def _(b):
                here = pl.ds(pl.multiple_of(b * BS, BS), BS)
                both = part[h, xx * 2 + c, here, :].astype(F32) + pair_in[h, xx, here, :].astype(F32)
                part[h, xx * 2 + c, here, :] = both.astype(BF16)

            if o:
                x_c[h, o].start()

    def dists(h):
        table, norm = (cent, cn_own) if h == 0 else (others, cn_oth)

        @pl.loop(0, owned)
        def _(b):
            pts = recv[h, b]
            tab = table[pl.ds(pl.multiple_of(b * BS, BS), BS), :]
            cross = lax.dot_general(pts, tab, (((1,), (1,)), ((), ())), preferred_element_type=F32)
            wide = pts.astype(F32)
            rn = jnp.sum(wide * wide, axis=1, keepdims=True)
            dist[h, b] = ((rn - 2.0 * cross + norm[pl.ds(b, 1), :]) / width).astype(BF16)

        for o in range(1, team):
            ret_c[h, o].start()
        own = pltpu.make_async_copy(dist.at[h, :, mine], ret.at[h, me], l_sem.at[h])
        own.start()
        own.wait()

    def total(h, here):
        acc = part[h, x * 2 + c, here, :].astype(F32)
        for o in range(1, n_x):
            acc += x_in[h, o - 1, here, :].astype(F32)
        return acc

    sums(1)
    pair(1)
    for j in range(n_cut):
        for o in range(1, n_grp):
            fwd[j * (n_grp - 1) + o - 1].wait_recv()
    cnc.wait_recv()
    dists(1)
    for o in range(1, n_x):
        x_c[1, o].wait_recv()

    @pl.loop(0, rows // BS)
    def _(b):
        here = pl.ds(pl.multiple_of(b * BS, BS), BS)
        fin[here, :] = total(1, here).astype(BF16)

    mid_c.start()
    sums(0)
    for o in range(1, n_grp):
        cnt_c[o].start()
    pair(0)
    dists(0)
    for o in range(1, n_grp):
        cnt_c[o].wait_recv()
    acc = cnt[...]
    for o in range(1, n_grp):
        acc += cnt_in[o - 1]
    cnt_fin[...] = acc
    cm_c.start()
    for h in (1, 0):
        for o in range(1, team):
            ret_c[h, o].wait_recv()

    ptile = min(256, npts)

    @pl.loop(0, npts // ptile)
    def _(t):
        here = pl.ds(pl.multiple_of(t * ptile, ptile), ptile)
        where = slot_col[here, :]
        acc = jnp.zeros((ptile, BS), F32)
        for h in range(2):
            for s in range(team):
                base = (s * 2 + h) * per
                hot = (lax.broadcasted_iota(jnp.int32, (ptile, per), 1) + base == where).astype(BF16)
                acc += jnp.dot(hot, ret[h, s].reshape(per, BS), preferred_element_type=F32)
        distances[here, :] = acc.astype(BF16)

    for o in range(1, n_x):
        x_c[0, o].wait_recv()
    mid_c.wait_recv()

    @pl.loop(0, rows // BS)
    def _(b):
        here = pl.ds(pl.multiple_of(b * BS, BS), BS)
        col_sums[here, :] = total(0, here) + mid_in[here, :].astype(F32)

    cm_c.wait_recv()
    counts_out[...] = cnt_fin[0] + cnt_mid[...]

    for q in cen + [cnc] + fwd + [mid_c, cm_c]:
        q.wait_send()
    for group in (pts_c, tgt_c, pair_c, x_c, ret_c, cnt_c):
        for q in group.values():
            q.wait_send()


def shards(points, blocks, finals, centroids):
    n_dev = lax.axis_size("dev")
    n_grp = lax.axis_size("grp")
    team = n_dev // 2
    half = lax.axis_index("dev") // team
    npoints, width = points.shape
    rows = centroids.shape[0]
    owned = rows // BS
    nblocks = owned * n_dev
    depth = 2 * npoints // nblocks
    share = width // n_grp
    piece = rows // n_grp
    n_x = n_grp // 2
    per = owned * depth

    block_ids = blocks[:, 0]
    labels = jnp.arange(nblocks, dtype=jnp.int32)
    member = block_ids[:, None] == labels[None, :]
    lower = (jnp.arange(npoints)[:, None] > jnp.arange(npoints)[None, :]).astype(BF16)
    before = jnp.dot(lower, member.astype(BF16), preferred_element_type=F32)
    ranks = jnp.sum(jnp.where(member, before, 0.0), axis=1).astype(jnp.int32)
    holder = block_ids // owned
    other = (holder // team) ^ half
    place = ((holder % team) * 2 + other) * owned + block_ids % owned
    slots = place * depth + ranks
    final_row = jnp.broadcast_to((finals + 1).astype(BF16)[None, :], (8, npoints))
    cn = jnp.sum(jnp.square(centroids.astype(F32)), axis=-1).reshape(owned, BS)

    dma = pltpu.SemaphoreType.DMA
    vm = pltpu.VMEM
    distances, col_sums, counts = pl.pallas_call(
        functools.partial(kernel, n_grp, n_dev, owned, depth),
        out_shape=(
            jax.ShapeDtypeStruct((npoints, BS), BF16),
            jax.ShapeDtypeStruct((rows, share), F32),
            jax.ShapeDtypeStruct((owned, BS), F32),
        ),
        in_specs=[pl.BlockSpec(memory_space=vm)] * 6,
        out_specs=(pl.BlockSpec(memory_space=vm),) * 3,
        scratch_shapes=[
            vm((2, team - 1, owned, depth, width), BF16),
            vm((2, owned, team * depth, width), BF16),
            vm((2, team - 1, 8, per), F32),
            vm((2, team - 1, 8, per), F32),
            vm((2, owned, team * depth, 8), F32),
            vm((rows, width), BF16),
            vm((owned, BS), F32),
            vm((2, n_grp, rows, share), BF16),
            vm((2, n_x, rows, share), BF16),
            vm((2, max(n_x - 1, 1), rows, share), BF16),
            vm((rows, share), BF16),
            vm((rows, share), BF16),
            vm((2, owned, team * depth, BS), BF16),
            vm((2, team, owned, depth, BS), BF16),
            vm((2, owned, BS), F32),
            vm((n_grp - 1, 2, owned, BS), F32),
            vm((2, owned, BS), F32),
            vm((owned, BS), F32),
            dma((2, team)), dma((2, team)), dma((2, team)), dma((2, team)),
            dma((2,)), dma((2,)), dma((2, n_grp)), dma((2, n_grp)), dma((1,)), dma((1,)),
            dma((2, n_x)), dma((2, n_x)), dma((2, n_x)), dma((2, n_x)),
            dma((1,)), dma((1,)), dma((n_grp,)), dma((n_grp,)), dma((1,)), dma((1,)),
            dma((2, team)), dma((2, team)), dma((2,)),
        ],
        compiler_params=pltpu.CompilerParams(
            collective_id=0, has_side_effects=True, vmem_limit_bytes=67_000_000
        ),
    )(slots[None, :], slots[:, None], final_row, points, centroids, cn)

    own_cols = lax.dynamic_slice_in_dim(centroids, lax.axis_index("grp") * share, share, 1).astype(F32)
    refreshed_centroids = (col_sums + own_cols) / (counts.reshape(rows) + 1.0)[:, None]
    return (distances, refreshed_centroids)


def solution(mesh):
    placed = (P(("grp", "dev"), None), P(("grp", "dev"), None), P(("grp", "dev")), P("dev", None))
    return jax.shard_map(
        shards,
        mesh=mesh,
        in_specs=placed,
        out_specs=(P(("grp", "dev"), None), P("dev", "grp")),
        check_vma=False,
    )
```

time: 340 us -> 202 us (0.59)
  waiting for transfers between devices: 222 us -> 0 us
  Pallas kernels: 0 us -> 185 us
  local copies, waits for them, and re-layouts: 48.4 us -> 3.42 us
  starting transfers between devices: 15.9 us -> 0 us
  matrix products: 18 us -> 2.56 us
  between operations: 14.1 us -> 0.73 us
  blocking collectives: 6.49 us -> 0 us
    all_to_all x3 -> x0, waiting for transfers between devices: 222 us -> none  [the longest x1 181 us: shards(): lax.all_to_all(outgoing, 'dev', split_axis=0, concat_axis=1, tiled=True)]
    pallas_call x0 -> x1, Pallas kernels: none -> 185 us  [shards(): pl.pallas_call(functools.partial(kernel, n_grp, n_dev, owned, depth), out...]
    scatter x2 -> x0, local copies, waits for them, and re-layouts: 23.5 us -> none  [the longest x1 15.2 us: shards(): jnp.zeros((nblocks * depth, width), jnp.bfloat16).at[slots].set(points)]
    all_to_all x3 -> x0, starting transfers between devices: 15.9 us -> none  [the longest x1 5.77 us: shards(): lax.all_to_all(targets, 'dev', split_axis=0, concat_axis=1, tiled=True)]
    dot_general x3 -> x1, matrix products: 18 us -> 2.56 us  [shards(): before = jnp.dot(lower, member.astype(BF16), preferred_element_type=F32)]
    all_to_all x5 -> x0, local copies, waits for them, and re-layouts: 11.1 us -> none  [the longest x1 8.39 us: shards(): lax.all_to_all(outgoing, 'dev', split_axis=0, concat_axis=1, tiled=True)]
    gather x1 -> x0, local copies, waits for them, and re-layouts: 9.06 us -> none  [shards(): distances = returned.reshape(nblocks * depth, block_size)[slots]]
    reduce_sum x3 -> x1, other arithmetic: 9.08 us -> 0.89 us  [shards(): cn = jnp.sum(jnp.square(centroids.astype(F32)), axis=-1).reshape(owned, BS)]
  transfers between devices with their start and end apart: 4 -> 0, of which waited for: 2 -> 0; matrix products, arithmetic and copies ran while one was open for 14% -> 0% of each run, Pallas kernels for 0% -> 0%
where the time goes in v2:
time: 202 us
  Pallas kernels  185 us (92%)
  other arithmetic  9.84 us (5%)
  local copies, waits for them, and re-layouts  3.42 us (2%)
  matrix products  2.56 us (1%)
    pallas_call x1, Pallas kernels, shards(): pl.pallas_call(functools.partial(kernel, n_grp, n_dev, owned, depth), out...  185 us

profile of v2, /device:TPU:5, one launch (start us, length us, event | category | flops | bytes accessed | tf_op | source)
XLA Modules:
  0.0 201.9 jit_solution(2716711733079019050)
XLA Ops:
  0.6 0.0 copy-start.2
  0.7 0.0 copy-start
  0.7 0.9 add_convert_fusion
  1.5 2.6 %fusion.2 = f32[2048]{0:T(1024)S(1)} fusion(s32[2048]{0:T(1024)} %bitcast.19), kind=kOutput, calls=%fused_computation.15 | convolution fusion | flops 541587456 | bytes 16384 | tf_op jit(solution)/shard_map/dot_general | solution.py:285
  4.1 0.0 copy-done.2
  4.1 0.7 multiply_add_fusion.slot_row
  4.8 0.0 copy-done
  4.8 0.9 multiply_reduce_fusion
  5.7 0.6 reshape.212.cn_own
  6.3 0.6 broadcast_in_dim.7.final_row
  7.0 0.5 copy.18
  7.4 0.4 copy.20
  7.8 0.4 copy.13
  8.2 3.0 %fusion.8.slot_col = s32[2048,1]{1,0:T(8,128)} fusion(s32[2048,1]{1,0:T(8,128)S(1)} %copy.20, pred[2048,1]{1,0:T(8,128)(4,1)S(1)} %copy.18, s32[2048,1]{1,0:T(8,128)S(1)} %copy.13, s32[]{:T(128)S(6)} %select_n.73), kind=kLoop, calls=%fused_computation.21 | loop fusion | flops 90112 | bytes 26628 | tf_op jit(solution)/shard_map/add | solution.py:290
  11.2 185.4 %shard_map.59 = (bf16[2048,256]{1,0:T(8,128)(2,1)}, f32[2048,256]{1,0:T(8,128)}, f32[8,256]{1,0:T(8,128)}) custom-call(s32[1,2048]{1,0:T(1,128)} %multiply_add_fusion.slot_row, s32[2048,1]{1,0:T(8,128)} %fusion.8.slot_col, bf16[8,2048]{1,0:T(8,128)(2,1)} %broadcast_in_dim.7.final_row, bf16[2048,1024]{1,0:T(8,128)(2,1)} %points.1, bf16[2048,1024]{1,0:T(8,128)(2,1)} %cent.1, ...), custom_call_target="tpu_custom_call" | custom-call | tf_op jit(solution)/shard_map/pallas_call | solution.py:296
  196.6 0.0 copy-start.1
  196.7 0.8 add_bitcast_fusion
  197.4 3.5 %add_divide_fusion = f32[2048,256]{1,0:T(8,128)} fusion(f32[2048,256]{1,0:T(8,128)} %get-tuple-element.6, f32[2048]{0:T(1024)S(1)} %bitcast.22, bf16[2048,1024]{1,0:T(8,128)(2,1)} %cent.1, s32[]{:T(128)S(6)} %select_n.80), kind=kLoop, calls=%fused_computation.4 | loop fusion | flops 1572864 | bytes 5251076 | tf_op jit(solution)/shard_map/div | solution.py:336
  201.0 0.0 copy-done.1
  201.0 1.0 copy.27
  (3 shorter events, 0.0 us)
Async XLA Ops:
  0.6 3.5 %copy-start.2 = (s32[2048,1]{0,1:T(1,128)S(1)}, s32[2048,1]{0,1:T(1,128)}, u32[]{:S(2)}) copy-start(s32[2048,1]{0,1:T(1,128)} %param.5) | copy-start | bytes 24580
  0.7 4.2 %copy-start = (bf16[2048,1024]{1,0:T(8,128)(2,1)S(1)}, bf16[2048,1024]{1,0:T(8,128)(2,1)}, u32[]{:S(2)}) copy-start(bf16[2048,1024]{1,0:T(8,128)(2,1)} %cent.1) | copy-start | bytes 12582916
  196.6 4.3 %copy-start.1 = (bf16[2048,256]{1,0:T(8,128)(2,1)S(1)}, bf16[2048,256]{1,0:T(8,128)(2,1)}, u32[]{:S(2)}) copy-start(bf16[2048,256]{1,0:T(8,128)(2,1)} %get-tuple-element.10) | copy-start | bytes 3145732

commit v3 on v2

--- a/solution.py
+++ b/solution.py
@@ -14,13 +14,13 @@
 
 def kernel(
     n_grp, n_dev, owned, depth,
-    slot_row, slot_col, final_row, points, cent, cn_own,
+    place_row, block_row, final_row, points_hbm, cent_hbm, cn_own,
     distances, col_sums, counts_out,
-    out, recv, tgt_out, tgt_in, tgt_col, others, cn_oth,
+    points, cent, slot_row, slot_col, out, recv, tgt_out, tgt_in, tgt_col, others, cn_oth,
     part, pair_in, x_in, fin, mid_in, dist, ret,
     cnt, cnt_in, cnt_fin, cnt_mid,
     s_pts, r_pts, s_tgt, r_tgt, s_cen, r_cen, s_fwd, r_fwd, s_cn, r_cn,
-    s_pair, r_pair, s_x, r_x, s_mid, r_mid, s_cnt, r_cnt, s_cm, r_cm, s_ret, r_ret, l_sem,
+    s_pair, r_pair, s_x, r_x, s_mid, r_mid, s_cnt, r_cnt, s_cm, r_cm, s_ret, r_ret, l_sem, in_sem,
 ):
     team = n_dev // 2
     n_x = n_grp // 2
@@ -48,6 +48,10 @@
             src_ref=src, dst_ref=dst, send_sem=ss, recv_sem=rs, device_id=dev, device_id_type=MESH
         )
 
+    load_points = pltpu.make_async_copy(points_hbm, points, in_sem.at[0])
+    load_cent = pltpu.make_async_copy(cent_hbm, cent, in_sem.at[1])
+    load_points.start()
+
     swap = to(g, (d + team) % n_dev)
     barrier = pltpu.get_barrier_semaphore()
     peers = [to(g, mate(o)) for o in range(1, team)] + [swap]
@@ -59,11 +63,29 @@
     def span(gg, j):
         return pl.ds(pl.multiple_of(gg * piece + j * pc, pc), pc)
 
-    cen = [copy(cent.at[span(g, j)], others.at[span(g, j)], s_cen.at[j], r_cen.at[j], swap) for j in range(n_cut)]
+    cen = [copy(cent_hbm.at[span(g, j)], others.at[span(g, j)], s_cen.at[j], r_cen.at[j], swap) for j in range(n_cut)]
     cnc = copy(cn_own, cn_oth, s_cn.at[0], r_cn.at[0], swap)
     for j in range(n_cut):
         cen[j].start()
     cnc.start()
+    load_cent.start()
+
+    n_blocks = owned * n_dev
+    step = min(256, npts)
+    before = (
+        lax.broadcasted_iota(jnp.int32, (step, step), 0) < lax.broadcasted_iota(jnp.int32, (step, step), 1)
+    ).astype(BF16)
+    seen = jnp.zeros((n_blocks, 1), F32)
+    for t in range(npts // step):
+        here = slice(t * step, (t + 1) * step)
+        member = (lax.broadcasted_iota(jnp.int32, (n_blocks, step), 0) == block_row[:, here]).astype(F32)
+        prior = jnp.dot(member.astype(BF16), before, preferred_element_type=F32) + seen
+        rank = jnp.sum(member * prior, axis=0, keepdims=True)
+        seen = seen + jnp.sum(member, axis=1, keepdims=True)
+        slot = place_row[:, here] * depth + rank.astype(jnp.int32)
+        slot_row[:, here] = slot
+        slot_col[here, :] = jnp.transpose(jnp.broadcast_to(slot.astype(F32), (8, step)))
+    load_points.wait()
 
     fwd = [
         copy(others.at[span(g, j)], others.at[span(g, j)], s_fwd.at[j, o], r_fwd.at[j, o], to((g + o) % n_grp, d))
@@ -86,7 +108,7 @@
             tgt_c[h, o] = copy(tgt_out.at[h, o - 1], tgt_in.at[h, o - 1], s_tgt.at[h, o], r_tgt.at[h, o], to(g, mate(o)))
 
     def pack_all(h):
-        for o in range(1, team):
+        for o in list(range(team // 2, team)) + list(range(1, team // 2)):
             for t in range(per // tile):
                 pts, tg = packed(h, (me + o) % team, t)
                 out[h, o - 1, t * nb : (t + 1) * nb] = pts
@@ -198,6 +220,7 @@
             acc += x_in[h, o - 1, here, :].astype(F32)
         return acc
 
+    load_cent.wait()
     sums(1)
     pair(1)
     for j in range(n_cut):
@@ -217,8 +240,8 @@
     sums(0)
     for o in range(1, n_grp):
         cnt_c[o].start()
+    dists(0)
     pair(0)
-    dists(0)
     for o in range(1, n_grp):
         cnt_c[o].wait_recv()
     acc = cnt[...]
@@ -226,24 +249,27 @@
         acc += cnt_in[o - 1]
     cnt_fin[...] = acc
     cm_c.start()
-    for h in (1, 0):
+    ptile = min(256, npts)
+
+    def gather(h):
         for o in range(1, team):
             ret_c[h, o].wait_recv()
 
-    ptile = min(256, npts)
-
-    @pl.loop(0, npts // ptile)
-    def _(t):
-        here = pl.ds(pl.multiple_of(t * ptile, ptile), ptile)
-        where = slot_col[here, :]
-        acc = jnp.zeros((ptile, BS), F32)
-        for h in range(2):
+        @pl.loop(0, npts // ptile)
+        def _(t):
+            here = pl.ds(pl.multiple_of(t * ptile, ptile), ptile)
+            where = slot_col[here, 0:1].astype(jnp.int32)
+            acc = jnp.zeros((ptile, BS), F32)
             for s in range(team):
                 base = (s * 2 + h) * per
                 hot = (lax.broadcasted_iota(jnp.int32, (ptile, per), 1) + base == where).astype(BF16)
                 acc += jnp.dot(hot, ret[h, s].reshape(per, BS), preferred_element_type=F32)
-        distances[here, :] = acc.astype(BF16)
-
+            if h == 0:
+                acc += distances[here, :].astype(F32)
+            distances[here, :] = acc.astype(BF16)
+
+    gather(1)
+    gather(0)
     for o in range(1, n_x):
         x_c[0, o].wait_recv()
     mid_c.wait_recv()
@@ -279,15 +305,9 @@
     per = owned * depth
 
     block_ids = blocks[:, 0]
-    labels = jnp.arange(nblocks, dtype=jnp.int32)
-    member = block_ids[:, None] == labels[None, :]
-    lower = (jnp.arange(npoints)[:, None] > jnp.arange(npoints)[None, :]).astype(BF16)
-    before = jnp.dot(lower, member.astype(BF16), preferred_element_type=F32)
-    ranks = jnp.sum(jnp.where(member, before, 0.0), axis=1).astype(jnp.int32)
     holder = block_ids // owned
     other = (holder // team) ^ half
     place = ((holder % team) * 2 + other) * owned + block_ids % owned
-    slots = place * depth + ranks
     final_row = jnp.broadcast_to((finals + 1).astype(BF16)[None, :], (8, npoints))
     cn = jnp.sum(jnp.square(centroids.astype(F32)), axis=-1).reshape(owned, BS)
 
@@ -300,9 +320,15 @@
             jax.ShapeDtypeStruct((rows, share), F32),
             jax.ShapeDtypeStruct((owned, BS), F32),
         ),
-        in_specs=[pl.BlockSpec(memory_space=vm)] * 6,
+        in_specs=[pl.BlockSpec(memory_space=vm)] * 3
+        + [pl.BlockSpec(memory_space=pl.ANY)] * 2
+        + [pl.BlockSpec(memory_space=vm)],
         out_specs=(pl.BlockSpec(memory_space=vm),) * 3,
         scratch_shapes=[
+            vm((npoints, width), BF16),
+            vm((rows, width), BF16),
+            vm((1, npoints), jnp.int32),
+            vm((npoints, 8), F32),
             vm((2, team - 1, owned, depth, width), BF16),
             vm((2, owned, team * depth, width), BF16),
             vm((2, team - 1, 8, per), F32),
@@ -325,12 +351,12 @@
             dma((2,)), dma((2,)), dma((2, n_grp)), dma((2, n_grp)), dma((1,)), dma((1,)),
             dma((2, n_x)), dma((2, n_x)), dma((2, n_x)), dma((2, n_x)),
             dma((1,)), dma((1,)), dma((n_grp,)), dma((n_grp,)), dma((1,)), dma((1,)),
-            dma((2, team)), dma((2, team)), dma((2,)),
+            dma((2, team)), dma((2, team)), dma((2,)), dma((2,)),
         ],
         compiler_params=pltpu.CompilerParams(
             collective_id=0, has_side_effects=True, vmem_limit_bytes=67_000_000
         ),
-    )(slots[None, :], slots[:, None], final_row, points, centroids, cn)
+    )(place[None, :], block_ids[None, :], final_row, points, centroids, cn)
 
     own_cols = lax.dynamic_slice_in_dim(centroids, lax.axis_index("grp") * share, share, 1).astype(F32)
     refreshed_centroids = (col_sums + own_cols) / (counts.reshape(rows) + 1.0)[:, None]

time: 202 us -> 196 us (0.970); the launches traced: 202 us -> 194 us
  Pallas kernels: 185 us -> 181 us
  matrix products: 2.56 us -> 0 us
    pallas_call x1, Pallas kernels: 185 us -> 181 us  [shards(): pl.pallas_call(functools.partial(kernel, n_grp, n_dev, owned, depth), out...]
    dot_general x1 -> x0, matrix products: 2.56 us -> none  [shards(): before = jnp.dot(lower, member.astype(BF16), preferred_element_type=F32)]
    add x2 -> x1, other arithmetic: 3.78 us -> 1.42 us  [shards(): place = (holder % team * 2 + other) * owned + block_ids % owned]
    reduce_sum x1, other arithmetic: 0.89 us -> 3.07 us  [shards(): cn = jnp.sum(jnp.square(centroids.astype(F32)), axis=-1).reshape(owned, BS)]
where the time goes in v3:
time: 196 us; the launch traced here: 194 us
  Pallas kernels  181 us (92%)
  other arithmetic  9.51 us (5%)
  local copies, waits for them, and re-layouts  2.2 us (1%)
    pallas_call x1, Pallas kernels, shards(): pl.pallas_call(functools.partial(kernel, n_grp, n_dev, owned, depth), out...  181 us

profile of v3, /device:TPU:5, one launch (start us, length us, event | category | flops | bytes accessed | tf_op | source)
XLA Modules:
  0.0 193.6 jit_solution(10313147875242247856)
XLA Ops:
  0.6 0.7 add_convert_fusion
  1.3 1.4 fusion.place_row
  2.8 3.1 %multiply_reduce_fusion = f32[2048]{0:T(1024)S(1)} fusion(bf16[2048,1024]{1,0:T(8,128)(2,1)} %cent_hbm.1), kind=kLoop, calls=%fused_computation | loop fusion | flops 6289408 | bytes 4202496 | tf_op jit(solution)/shard_map/reduce_sum | solution.py:312
  5.8 0.6 reshape.190.cn_own
  6.4 0.6 broadcast_in_dim.2.final_row
  7.1 181.2 %shard_map.59 = (bf16[2048,256]{1,0:T(8,128)(2,1)}, f32[2048,256]{1,0:T(8,128)}, f32[8,256]{1,0:T(8,128)}) custom-call(s32[1,2048]{1,0:T(1,128)} %fusion.place_row, s32[1,2048]{1,0:T(1,128)} %bitcast.5, bf16[8,2048]{1,0:T(8,128)(2,1)} %broadcast_in_dim.2.final_row, bf16[2048,1024]{1,0:T(8,128)(2,1)} %points_hbm.1, bf16[2048,1024]{1,0:T(8,128)(2,1)} %cent_hbm.1, ...), custom_call_target="tpu_custom_call" | custom-call | tf_op jit(solution)/shard_map/pallas_call | solution.py:316
  188.3 0.7 add_bitcast_fusion
  189.0 0.0 copy-start
  189.0 3.6 %add_divide_fusion = f32[2048,256]{1,0:T(8,128)} fusion(f32[2048,256]{1,0:T(8,128)} %get-tuple-element.6, f32[2048]{0:T(1024)S(1)} %bitcast.6, bf16[2048,1024]{1,0:T(8,128)(2,1)} %cent_hbm.1, s32[]{:T(128)S(6)} %select_n.59), kind=kLoop, calls=%fused_computation.1 | loop fusion | flops 1572864 | bytes 5251076 | tf_op jit(solution)/shard_map/div | solution.py:362
  192.6 0.0 copy-done
  192.6 1.0 copy.8
  (1 shorter events, 0.0 us)
Async XLA Ops:
  189.0 3.6 %copy-start = (bf16[2048,256]{1,0:T(8,128)(2,1)S(1)}, bf16[2048,256]{1,0:T(8,128)(2,1)}, u32[]{:S(2)}) copy-start(bf16[2048,256]{1,0:T(8,128)(2,1)} %get-tuple-element.10) | copy-start | bytes 3145732
